TPU v7x, 32 devices: a whole 2x2x4 slice. The times are simulated.
32 devices in a mesh: seq: 8 (over z, core), feat: 4 (over y, x).
Axes of the slice: x: 2, y: 2, z: 4, core: 2. Of those that a mesh axis runs over, the one named last changes fastest.
Arguments:
- activations: bfloat16 [2048, 6144], P('seq', 'feat'), may hold values from -15 to 15
- ridge_scale: float32 [], replicated, may hold values from 0.5 to 2
Outputs:
- whitened: bfloat16 [2048, 6144], P('seq', 'feat')
All inputs are finite; a program needn't handle non-finite values.
Results may differ from a plain program's by a relative error of at most 0.0033.
Values sent between devices are 32-bit elements; how exact they have to be, the bound alone decides.
A program may use at most 128 MiB of HBM per device.

v0:
```python
import functools

import jax
import jax.numpy as jnp
from jax import lax
from jax.experimental import pallas as pl
from jax.experimental.pallas import tpu as pltpu
from jax.sharding import PartitionSpec as P

RANK = 128
ROOT_STEPS = 12
PANEL = 16
MESH = pl.DeviceIdType.MESH
HIGHEST = lax.Precision.HIGHEST


def mm(a, b):
    return jnp.dot(a, b, precision=HIGHEST, preferred_element_type=jnp.float32)


def mm_t(a, b):
    return lax.dot_general(
        a, b, (((1,), (1,)), ((), ())), precision=HIGHEST, preferred_element_type=jnp.float32
    )


def split_3(x):
    high = x.astype(jnp.bfloat16)
    rest = x - high.astype(jnp.float32)
    middle = rest.astype(jnp.bfloat16)
    low = (rest - middle.astype(jnp.float32)).astype(jnp.bfloat16)
    return high, middle, low


def eye():
    rows = lax.broadcasted_iota(jnp.int32, (RANK, RANK), 0)
    columns = lax.broadcasted_iota(jnp.int32, (RANK, RANK), 1)
    return jnp.where(rows == columns, 1.0, 0.0).astype(jnp.float32)


def trace(matrix):
    size = matrix.shape[0]
    rows = lax.broadcasted_iota(jnp.int32, (size, size), 0)
    columns = lax.broadcasted_iota(jnp.int32, (size, size), 1)
    kept = jnp.where(rows == columns, matrix, 0.0)
    return jnp.sum(jnp.sum(kept, axis=1, keepdims=True), axis=0, keepdims=True)


def factorize(matrices, work, inverse=True):
    count = len(matrices)
    for k in range(count):
        work[k, :, :RANK] = matrices[k]
        if inverse:
            work[k, :, RANK:] = eye()
    lane = lax.broadcasted_iota(jnp.int32, (PANEL, RANK), 1)
    sub = lax.broadcasted_iota(jnp.int32, (PANEL, RANK), 0)

    def step(index, carry):
        first = pl.multiple_of(index * PANEL, PANEL)
        left = [work[k, pl.ds(first, PANEL), :RANK] for k in range(count)]
        right = [work[k, pl.ds(first, PANEL), RANK:] for k in range(count) if inverse]
        columns = [
            [
                jnp.broadcast_to(
                    jnp.sum(jnp.where(lane == first + c, left[k], 0.0), axis=1, keepdims=True),
                    (PANEL, RANK),
                )
                for c in range(PANEL)
            ]
            for k in range(count)
        ]
        for i in range(PANEL):
            for k in range(count):
                scale = lax.rsqrt(columns[k][i][i : i + 1, :])
                factor = jnp.where(sub > i, columns[k][i], 0.0) * scale
                for c in range(i + 1, PANEL):
                    columns[k][c] -= factor * (columns[k][c][i : i + 1, :] * scale)
                row_left = left[k][i : i + 1, :] * scale
                left[k] = jnp.where(sub == i, row_left, left[k] - factor * row_left)
                if inverse:
                    row_right = right[k][i : i + 1, :] * scale
                    right[k] = jnp.where(sub == i, row_right, right[k] - factor * row_right)
        for k in range(count):
            work[k, pl.ds(first, PANEL), :RANK] = left[k]
            if inverse:
                work[k, pl.ds(first, PANEL), RANK:] = right[k]
            h, m, l = split_3(jnp.where(lane >= first + PANEL, left[k], 0.0))
            sides = [split_3(side) for side in ([left[k], right[k]] if inverse else [left[k]])]
            h, m, l = (part.astype(jnp.float32) for part in (h, m, l))
            lhs = jnp.concatenate([h, h, m, m, h, l, jnp.zeros((2 * PANEL, RANK), jnp.float32)], axis=0)
            lhs = lhs.T.astype(jnp.bfloat16)
            for part, (a, b, c) in enumerate(sides):
                rhs = jnp.concatenate([a, b, a, b, c, a, jnp.zeros((2 * PANEL, RANK), jnp.bfloat16)], axis=0)
                work[k, :, part * RANK : (part + 1) * RANK] -= jnp.dot(
                    lhs, rhs, preferred_element_type=jnp.float32
                )
        return carry

    lax.fori_loop(0, RANK // PANEL, step, 0)
    rows = lax.broadcasted_iota(jnp.int32, (RANK, RANK), 0)
    cols = lax.broadcasted_iota(jnp.int32, (RANK, RANK), 1)
    return [
        (jnp.where(cols >= rows, work[k, :, :RANK], 0.0), work[k, :, RANK:] if inverse else None)
        for k in range(count)
    ]


def reduce_grams(grams, work):
    images = [(gram[:RANK, :] + gram[RANK:, :]) * 0.7071067811865476 for gram in grams]
    factors = factorize([mm_t(image, image) for image in images], work)
    bases = [mm(inverse, image) for (_, inverse), image in zip(factors, images)]
    quotients = [mm_t(mm(basis, gram), basis) for basis, gram in zip(bases, grams)]
    quotients = [0.5 * (quotient + quotient.T) for quotient in quotients]
    tails = [(trace(gram) - trace(quotient)) / RANK for gram, quotient in zip(grams, quotients)]
    uppers = [upper for upper, _ in factorize(quotients, work, False)]
    factors = factorize([mm_t(u, u) + tail * eye() for u, tail in zip(uppers, tails)], work)
    out = []
    for (_, inverse), upper, basis, gram in zip(factors, uppers, bases, grams):
        mixing = mm(mm(inverse, upper), basis)
        out.append((mixing, mm_t(mm(mixing, gram), mixing)))
    return out


def kernel(levels, feats, ridge_ref, rows_ref, out_ref, *scratch):
    work, tree, prefix, partner = scratch[:4]
    slab_slots = scratch[4]
    level_slots = scratch[5 : 5 + levels]
    last_slots = scratch[5 + levels]
    send_sem, recv_sem, pair_send, pair_recv = scratch[6 + levels :]
    seq = lax.axis_index("seq")
    feat = lax.axis_index("feat")
    width = rows_ref.shape[1]

    def bit_of(level):
        return lax.rem(seq // (1 << level), 2)

    def sibling(level):
        return seq + (1 << level) - 2 * (1 << level) * bit_of(level)

    barrier = pltpu.get_barrier_semaphore()
    for offset in range(1, feats):
        pl.semaphore_signal(
            barrier, inc=1, device_id=(seq, lax.rem(feat + offset, feats)), device_id_type=MESH
        )
    for level in range(levels):
        pl.semaphore_signal(
            barrier, inc=1, device_id=(sibling(level), feat), device_id_type=MESH
        )
    pl.semaphore_wait(barrier, feats - 1 + levels)

    def send_sum(slots, phase):
        copies = []
        for offset in range(1, feats):
            copy = pltpu.make_async_remote_copy(
                src_ref=slots.at[feat],
                dst_ref=slots.at[feat],
                send_sem=send_sem.at[phase, offset],
                recv_sem=recv_sem.at[phase, offset],
                device_id=(seq, lax.rem(feat + offset, feats)),
                device_id_type=MESH,
            )
            copy.start()
            copies.append(copy)
        return copies

    def finish_sum(slots, copies):
        for copy in copies:
            copy.wait()
        total = slots[0]
        for index in range(1, feats):
            total = total + slots[index]
        return total

    def fetch(level):
        for index, hop in enumerate(range(level, -1, -1)):
            source = tree if hop == level else partner
            bits = hop if hop == level else hop + 1
            size = RANK >> bits
            first = 0
            for bit in range(bits):
                first = first + bit_of(bit) * (RANK >> (bit + 1))
            span = pl.ds(pl.multiple_of(first, size), size) if bits else pl.ds(0, RANK)
            copy = pltpu.make_async_remote_copy(
                src_ref=source.at[level, span],
                dst_ref=partner.at[level, span],
                send_sem=pair_send.at[level, index],
                recv_sem=pair_recv.at[level, index],
                device_id=(sibling(hop), feat),
                device_id_type=MESH,
            )
            copy.start()
            copy.wait()

    rows = rows_ref[...]
    slab_slots[feat] = lax.dot_general(
        rows, rows, (((1,), (1,)), ((), ())), preferred_element_type=jnp.float32
    )
    gram = finish_sum(slab_slots, send_sum(slab_slots, 0))
    ((mixing, own_gram),) = reduce_grams([gram], work)
    h, m, l = split_3(mixing)
    sketch = (
        jnp.dot(l, rows, preferred_element_type=jnp.float32)
        + jnp.dot(m, rows, preferred_element_type=jnp.float32)
        + jnp.dot(h, rows, preferred_element_type=jnp.float32)
    )
    tree[0, :, :width] = sketch
    tree[0, :, width:] = own_gram
    prefix[...] = sketch
    prefix_gram = own_gram

    for level in range(levels):
        fetch(level)
        slots = level_slots[level]
        with_prefix = level > 0
        with_tree = level + 1 < levels or level == 0
        lefts = []
        if with_tree:
            lefts.append((tree.at[level, :, :width], tree[level, :, width:]))
        if with_prefix:
            lefts.append((prefix, prefix_gram))
        for index, (left, _) in enumerate(lefts):
            slots[feat, index * RANK : (index + 1) * RANK, :] = mm_t(
                left[...], partner[level, :, :width]
            )
        crosses = finish_sum(slots, send_sum(slots, 1 + level))
        other = partner[level, :, width:]
        stacked = []
        for index, (_, left_gram) in enumerate(lefts):
            cross = crosses[index * RANK : (index + 1) * RANK]
            stacked.append(
                jnp.concatenate(
                    [
                        jnp.concatenate([left_gram, cross], 1),
                        jnp.concatenate([cross.T, other], 1),
                    ],
                    0,
                )
            )
        results = reduce_grams(stacked, work)
        merged = []
        for (left, _), (mixing, new_gram) in zip(lefts, results):
            merged.append(
                (mm(mixing[:, :RANK], left[...]) + mm(mixing[:, RANK:], partner[level, :, :width]), new_gram)
            )
        keep = bit_of(level) == 1
        prefix[...] = jnp.where(keep, merged[-1][0], prefix[...])
        prefix_gram = jnp.where(keep, merged[-1][1], prefix_gram)
        if level + 1 < levels:
            tree[level + 1, :, :width] = merged[0][0]
            tree[level + 1, :, width:] = merged[0][1]

    ridge = ridge_ref[0, 0]
    seen_rows = ((seq + 1) * rows_ref.shape[0]).astype(jnp.float32)
    seen = jnp.full((1, 1), seen_rows * ridge, jnp.float32)
    half_basis = (prefix[...] * lax.rsqrt(seen)).astype(jnp.bfloat16)
    last_slots[feat] = lax.dot_general(
        rows, half_basis, (((1,), (1,)), ((), ())), preferred_element_type=jnp.float32
    )
    copies = send_sum(last_slots, 1 + levels)
    shifted = eye() + prefix_gram / seen
    norm = jnp.sqrt(
        jnp.sum(jnp.sum(shifted * shifted, axis=1, keepdims=True), axis=0, keepdims=True)
    )

    work[0, :, :RANK] = shifted / norm
    work[0, :, RANK:] = eye()

    def root_step(index, carry):
        current, other = work[0, :, :RANK], work[0, :, RANK:]
        middle = 1.5 * eye() - 0.5 * mm(other, current)
        work[0, :, :RANK] = mm(current, middle)
        work[0, :, RANK:] = mm(middle, other)
        return carry

    lax.fori_loop(0, ROOT_STEPS, root_step, 0)
    current = work[0, :, :RANK]
    total_gram = shifted + current * jnp.sqrt(norm)
    total_gram = 0.5 * (total_gram + total_gram.T)
    ((_, inverse),) = factorize([total_gram], work)
    projection = finish_sum(last_slots, copies)
    coefficients = mm(mm_t(projection, inverse), inverse).astype(jnp.bfloat16)
    restored = jnp.dot(coefficients, half_basis, preferred_element_type=jnp.float32)
    out_ref[...] = (
        (rows.astype(jnp.float32) - restored) * lax.rsqrt(jnp.full((1, 1), ridge, jnp.float32))
    ).astype(jnp.bfloat16)


def on_device(activations, ridge_scale):
    tokens, width = activations.shape
    feats = lax.axis_size("feat")
    levels = lax.axis_size("seq").bit_length() - 1
    wide = (RANK, width)
    f32 = jnp.float32
    scratch = [
        pltpu.VMEM((2, RANK, 2 * RANK), f32),
        pltpu.VMEM((levels, RANK, width + RANK), f32),
        pltpu.VMEM(wide, f32),
        pltpu.VMEM((levels, RANK, width + RANK), f32),
        pltpu.VMEM((feats, tokens, tokens), f32),
    ]
    for level in range(levels):
        count = 2 if 0 < level < levels - 1 else 1
        scratch.append(pltpu.VMEM((feats, count * RANK, RANK), f32))
    scratch.append(pltpu.VMEM((feats, tokens, RANK), f32))
    scratch += [
        pltpu.SemaphoreType.DMA((levels + 2, feats)),
        pltpu.SemaphoreType.DMA((levels + 2, feats)),
        pltpu.SemaphoreType.DMA((levels, levels)),
        pltpu.SemaphoreType.DMA((levels, levels)),
    ]
    return pl.pallas_call(
        functools.partial(kernel, levels, feats),
        out_shape=jax.ShapeDtypeStruct(activations.shape, activations.dtype),
        in_specs=[
            pl.BlockSpec(memory_space=pltpu.SMEM),
            pl.BlockSpec(memory_space=pltpu.VMEM),
        ],
        out_specs=pl.BlockSpec(memory_space=pltpu.VMEM),
        scratch_shapes=scratch,
        compiler_params=pltpu.CompilerParams(
            collective_id=0, has_side_effects=True, vmem_limit_bytes=60 * 1024 * 1024
        ),
    )(ridge_scale.reshape(1, 1), activations)


def solution(mesh):
    placed = (P("seq", "feat"), P())
    return jax.shard_map(
        on_device, mesh=mesh, in_specs=placed, out_specs=P("seq", "feat"), check_vma=False
    )
```

profile of v0, /device:TPU:0, one launch (start us, length us, event | category | flops | bytes accessed | tf_op | source)
XLA Modules:
  0.0 156.4 jit_solution(8615627440963282146)
XLA Ops:
  0.7 153.7 %shard_map.28 = bf16[256,1536]{1,0:T(8,128)(2,1)} custom-call(f32[1,1]{1,0:T(1,128)} %bitcast.1.ridge_ref, bf16[256,1536]{1,0:T(8,128)(2,1)} %rows_ref.1), custom_call_target="tpu_custom_call" | custom-call | tf_op jit(solution)/shard_map/pallas_call | solution.py:311
  154.4 2.1 %copy.5 = bf16[256,1536]{1,0:T(8,128)(2,1)} copy(bf16[256,1536]{1,0:T(8,128)(2,1)} %shard_map.28) | data formatting | bytes 1572864
where the time goes:
time: 157 us; the launch traced here: 156 us
  Pallas kernels  154 us (98%)
  local copies, waits for them, and re-layouts  2.06 us (1%)
    pallas_call x1, Pallas kernels, on_device(): pl.pallas_call(functools.partial(kernel, levels, feats), out_shape=jax.Sh...  154 us

commit v1 on v0

--- a/solution.py
+++ b/solution.py
@@ -9,7 +9,8 @@
 
 RANK = 128
 ROOT_STEPS = 12
-PANEL = 16
+BLOCK = 32
+SUB = 16
 MESH = pl.DeviceIdType.MESH
 HIGHEST = lax.Precision.HIGHEST
 
@@ -50,73 +51,113 @@
     count = len(matrices)
     for k in range(count):
         work[k, :, :RANK] = matrices[k]
-        if inverse:
-            work[k, :, RANK:] = eye()
-    lane = lax.broadcasted_iota(jnp.int32, (PANEL, RANK), 1)
-    sub = lax.broadcasted_iota(jnp.int32, (PANEL, RANK), 0)
+    lane = lax.broadcasted_iota(jnp.int32, (8, RANK), 1)
+    sub = lax.broadcasted_iota(jnp.int32, (8, RANK), 0)
+    rows = lax.broadcasted_iota(jnp.int32, (RANK, RANK), 0)
+    cols_i = lax.broadcasted_iota(jnp.int32, (RANK, RANK), 1)
+    groups = BLOCK // 8
 
     def step(index, carry):
-        first = pl.multiple_of(index * PANEL, PANEL)
-        left = [work[k, pl.ds(first, PANEL), :RANK] for k in range(count)]
-        right = [work[k, pl.ds(first, PANEL), RANK:] for k in range(count) if inverse]
-        columns = [
-            [
-                jnp.broadcast_to(
-                    jnp.sum(jnp.where(lane == first + c, left[k], 0.0), axis=1, keepdims=True),
-                    (PANEL, RANK),
-                )
-                for c in range(PANEL)
+        first = pl.multiple_of(index * BLOCK, BLOCK)
+        here = lane - first
+        left = [[work[k, pl.ds(first + 8 * g, 8), :RANK] for g in range(groups)] for k in range(count)]
+        for start in range(0, BLOCK, SUB):
+            active = range(start // 8, groups)
+            columns = [
+                [
+                    {
+                        g: jnp.broadcast_to(
+                            jnp.sum(jnp.where(here == start + c, left[k][g], 0.0), axis=1, keepdims=True),
+                            (8, RANK),
+                        )
+                        for g in active
+                        if 8 * g + 7 >= start + c
+                    }
+                    for c in range(SUB)
+                ]
+                for k in range(count)
             ]
-            for k in range(count)
-        ]
-        for i in range(PANEL):
+            if inverse:
+                inside = (here >= start) & (here < start + SUB)
+                for k in range(count):
+                    for g in active:
+                        unit = jnp.where(here == sub + 8 * g, 1.0, 0.0)
+                        left[k][g] = jnp.where(inside, unit, left[k][g])
+            for i in range(0, SUB, 2):
+                at, row = divmod(start + i, 8)
+                for k in range(count):
+                    one, two = columns[k][i], columns[k][i + 1]
+                    a = one[at][row : row + 1]
+                    b = one[at][row + 1 : row + 2]
+                    c = two[at][row + 1 : row + 2]
+                    det = a * c - b * b
+                    scale = lax.rsqrt(det)
+                    inv = scale * scale
+                    root = lax.rsqrt(a)
+                    up, down = left[k][at][row : row + 1], left[k][at][row + 1 : row + 2]
+                    for g in active:
+                        if g < at or (g == at and row == 6):
+                            continue
+                        u = (c * one[g] - b * two[g]) * inv
+                        v = (a * two[g] - b * one[g]) * inv
+                        for j in range(i + 2, SUB):
+                            if 8 * g + 7 >= start + j:
+                                to, spot = divmod(start + j, 8)
+                                columns[k][j][g] = columns[k][j][g] - (
+                                    u * one[to][spot : spot + 1] + v * two[to][spot : spot + 1]
+                                )
+                        if g == at:
+                            u = jnp.where(sub > row + 1, u, 0.0)
+                            v = jnp.where(sub > row + 1, v, 0.0)
+                        left[k][g] = left[k][g] - (u * up + v * down)
+                    down = (a * down - b * up) * (root * scale)
+                    left[k][at] = jnp.where(
+                        sub == row, up * root, jnp.where(sub == row + 1, down, left[k][at])
+                    )
+        for k in range(count):
+            if inverse:
+                for g in range(SUB // 8):
+                    left[k][g] = jnp.where((here >= SUB) & (here < BLOCK), 0.0, left[k][g])
+            for g in range(groups):
+                work[k, pl.ds(first + 8 * g, 8), :RANK] = left[k][g]
+
+        @pl.when(index < RANK // BLOCK - 1)
+        def _():
             for k in range(count):
-                scale = lax.rsqrt(columns[k][i][i : i + 1, :])
-                factor = jnp.where(sub > i, columns[k][i], 0.0) * scale
-                for c in range(i + 1, PANEL):
-                    columns[k][c] -= factor * (columns[k][c][i : i + 1, :] * scale)
-                row_left = left[k][i : i + 1, :] * scale
-                left[k] = jnp.where(sub == i, row_left, left[k] - factor * row_left)
+                whole = jnp.concatenate(left[k], axis=0)
+                wide = lax.broadcasted_iota(jnp.int32, (BLOCK, RANK), 1)
+                a, b, c = split_3(whole)
+                h, m, l = (jnp.where(wide >= first + BLOCK, part.astype(jnp.float32), 0.0) for part in (a, b, c))
+                lhs = jnp.concatenate([h, h, m, m, h, l, jnp.zeros((2 * BLOCK, RANK), jnp.float32)], axis=0)
+                lhs = lhs.T.astype(jnp.bfloat16)
+                rhs = jnp.concatenate([a, b, a, b, c, a, jnp.zeros((2 * BLOCK, RANK), jnp.bfloat16)], axis=0)
+                update = jnp.dot(lhs, rhs, preferred_element_type=jnp.float32)
+                old = work[k, :, :RANK]
                 if inverse:
-                    row_right = right[k][i : i + 1, :] * scale
-                    right[k] = jnp.where(sub == i, row_right, right[k] - factor * row_right)
-        for k in range(count):
-            work[k, pl.ds(first, PANEL), :RANK] = left[k]
-            if inverse:
-                work[k, pl.ds(first, PANEL), RANK:] = right[k]
-            h, m, l = split_3(jnp.where(lane >= first + PANEL, left[k], 0.0))
-            sides = [split_3(side) for side in ([left[k], right[k]] if inverse else [left[k]])]
-            h, m, l = (part.astype(jnp.float32) for part in (h, m, l))
-            lhs = jnp.concatenate([h, h, m, m, h, l, jnp.zeros((2 * PANEL, RANK), jnp.float32)], axis=0)
-            lhs = lhs.T.astype(jnp.bfloat16)
-            for part, (a, b, c) in enumerate(sides):
-                rhs = jnp.concatenate([a, b, a, b, c, a, jnp.zeros((2 * PANEL, RANK), jnp.bfloat16)], axis=0)
-                work[k, :, part * RANK : (part + 1) * RANK] -= jnp.dot(
-                    lhs, rhs, preferred_element_type=jnp.float32
-                )
+                    inside = (cols_i >= first) & (cols_i < first + BLOCK) & (rows >= first + BLOCK)
+                    old = jnp.where(inside, 0.0, old)
+                work[k, :, :RANK] = old - update
         return carry
 
-    lax.fori_loop(0, RANK // PANEL, step, 0)
-    rows = lax.broadcasted_iota(jnp.int32, (RANK, RANK), 0)
-    cols = lax.broadcasted_iota(jnp.int32, (RANK, RANK), 1)
-    return [
-        (jnp.where(cols >= rows, work[k, :, :RANK], 0.0), work[k, :, RANK:] if inverse else None)
-        for k in range(count)
-    ]
+    lax.fori_loop(0, RANK // BLOCK, step, 0)
+    if inverse:
+        return [jnp.where(cols_i <= rows, work[k, :, :RANK], 0.0) for k in range(count)]
+    return [jnp.where(cols_i >= rows, work[k, :, :RANK], 0.0) for k in range(count)]
 
 
 def reduce_grams(grams, work):
-    images = [(gram[:RANK, :] + gram[RANK:, :]) * 0.7071067811865476 for gram in grams]
-    factors = factorize([mm_t(image, image) for image in images], work)
-    bases = [mm(inverse, image) for (_, inverse), image in zip(factors, images)]
-    quotients = [mm_t(mm(basis, gram), basis) for basis, gram in zip(bases, grams)]
-    quotients = [0.5 * (quotient + quotient.T) for quotient in quotients]
-    tails = [(trace(gram) - trace(quotient)) / RANK for gram, quotient in zip(grams, quotients)]
-    uppers = [upper for upper, _ in factorize(quotients, work, False)]
-    factors = factorize([mm_t(u, u) + tail * eye() for u, tail in zip(uppers, tails)], work)
+    scaled = [gram * (1.0 / trace(gram)) for gram in grams]
+    images = [(gram[:RANK, :] + gram[RANK:, :]) * 0.7071067811865476 for gram in scaled]
+    inverses = factorize([mm_t(image, image) for image in images], work)
+    bases = [mm(inverse, image) for inverse, image in zip(inverses, images)]
+    quotients = [mm_t(mm(basis, gram), basis) for basis, gram in zip(bases, scaled)]
+    tails = [(trace(gram) - trace(quotient)) / RANK for gram, quotient in zip(scaled, quotients)]
+    uppers = factorize(quotients, work, False)
+    turned = [mm(upper, basis) for upper, basis in zip(uppers, bases)]
+    inverses = factorize([mm_t(u, u) + tail * eye() for u, tail in zip(uppers, tails)], work)
     out = []
-    for (_, inverse), upper, basis, gram in zip(factors, uppers, bases, grams):
-        mixing = mm(mm(inverse, upper), basis)
+    for inverse, turn, gram in zip(inverses, turned, grams):
+        mixing = mm(inverse, turn)
         out.append((mixing, mm_t(mm(mixing, gram), mixing)))
     return out
 
@@ -276,7 +317,7 @@
     current = work[0, :, :RANK]
     total_gram = shifted + current * jnp.sqrt(norm)
     total_gram = 0.5 * (total_gram + total_gram.T)
-    ((_, inverse),) = factorize([total_gram], work)
+    (inverse,) = factorize([total_gram], work)
     projection = finish_sum(last_slots, copies)
     coefficients = mm(mm_t(projection, inverse), inverse).astype(jnp.bfloat16)
     restored = jnp.dot(coefficients, half_basis, preferred_element_type=jnp.float32)

time: 157 us -> 140 us (0.89)
  Pallas kernels: 154 us -> 137 us
    pallas_call x1, Pallas kernels: 154 us -> 137 us  [on_device(): pl.pallas_call(functools.partial(kernel, levels, feats), out_shape=jax.Sh...]
where the time goes in v1:
time: 140 us; the launch traced here: 139 us
  Pallas kernels  137 us (98%)
  local copies, waits for them, and re-layouts  2.06 us (1%)
    pallas_call x1, Pallas kernels, on_device(): pl.pallas_call(functools.partial(kernel, levels, feats), out_shape=jax.Sh...  137 us

profile of v1, /device:TPU:0, one launch (start us, length us, event | category | flops | bytes accessed | tf_op | source)
XLA Modules:
  0.0 139.4 jit_solution(12649745391010775026)
XLA Ops:
  0.7 136.6 %shard_map.28 = bf16[256,1536]{1,0:T(8,128)(2,1)} custom-call(f32[1,1]{1,0:T(1,128)} %bitcast.1.ridge_ref, bf16[256,1536]{1,0:T(8,128)(2,1)} %rows_ref.1), custom_call_target="tpu_custom_call" | custom-call | tf_op jit(solution)/shard_map/pallas_call | solution.py:352
  137.3 2.1 %copy.5 = bf16[256,1536]{1,0:T(8,128)(2,1)} copy(bf16[256,1536]{1,0:T(8,128)(2,1)} %shard_map.28) | data formatting | bytes 1572864

commit v2 on v1

--- a/solution.py
+++ b/solution.py
@@ -145,10 +145,12 @@
     return [jnp.where(cols_i >= rows, work[k, :, :RANK], 0.0) for k in range(count)]
 
 
-def reduce_grams(grams, work):
+def reduce_grams(grams, work, between=None):
     scaled = [gram * (1.0 / trace(gram)) for gram in grams]
     images = [(gram[:RANK, :] + gram[RANK:, :]) * 0.7071067811865476 for gram in scaled]
     inverses = factorize([mm_t(image, image) for image in images], work)
+    if between is not None:
+        between()
     bases = [mm(inverse, image) for inverse, image in zip(inverses, images)]
     quotients = [mm_t(mm(basis, gram), basis) for basis, gram in zip(bases, scaled)]
     tails = [(trace(gram) - trace(quotient)) / RANK for gram, quotient in zip(scaled, quotients)]
@@ -162,32 +164,89 @@
     return out
 
 
-def kernel(levels, feats, ridge_ref, rows_ref, out_ref, *scratch):
-    work, tree, prefix, partner = scratch[:4]
-    slab_slots = scratch[4]
-    level_slots = scratch[5 : 5 + levels]
-    last_slots = scratch[5 + levels]
-    send_sem, recv_sem, pair_send, pair_recv = scratch[6 + levels :]
+def mix_rows(mixing, rows):
+    h, m, l = split_3(mixing)
+    return (
+        jnp.dot(l, rows, preferred_element_type=jnp.float32)
+        + jnp.dot(m, rows, preferred_element_type=jnp.float32)
+        + jnp.dot(h, rows, preferred_element_type=jnp.float32)
+    )
+
+
+def stack(first, cross, last):
+    return jnp.concatenate(
+        [jnp.concatenate([first, cross], 1), jnp.concatenate([cross.T, last], 1)], 0
+    )
+
+
+def fold(gram):
+    rows = lax.broadcasted_iota(jnp.int32, (RANK, RANK), 0)
+    columns = lax.broadcasted_iota(jnp.int32, (RANK, RANK), 1)
+    first, last = gram[:RANK, :RANK], gram[RANK:, RANK:]
+    both = jnp.where(columns <= rows, first, last)
+    diagonal = jnp.sum(jnp.where(columns == rows, last, 0.0), axis=0, keepdims=True)
+    return both, gram[:RANK, RANK:], jnp.broadcast_to(diagonal, (8, RANK))
+
+
+def unfold(both, cross, diagonal):
+    rows = lax.broadcasted_iota(jnp.int32, (RANK, RANK), 0)
+    columns = lax.broadcasted_iota(jnp.int32, (RANK, RANK), 1)
+    turned = both.T
+    first = jnp.where(columns <= rows, both, turned)
+    last = jnp.where(columns > rows, both, jnp.where(columns < rows, turned, diagonal))
+    return stack(first, cross, last)
+
+
+def kernel(levels, feats, names, ridge_ref, rows_ref, out_ref, *scratch):
+    at = dict(zip(names, scratch))
+    work, tree, partner, prefix = at["work"], at["tree"], at["partner"], at["prefix"]
+    prefix_gram, lower = at["prefix_gram"], at["lower"]
+    send_sem, recv_sem = at["send_sem"], at["recv_sem"]
+    pair_send, pair_recv = at["pair_send"], at["pair_recv"]
+    core_send, core_recv = at["core_send"], at["core_recv"]
+    up_send, up_recv = at["up_send"], at["up_recv"]
+    share_send, share_recv = at["share_send"], at["share_recv"]
     seq = lax.axis_index("seq")
     feat = lax.axis_index("feat")
     width = rows_ref.shape[1]
+    top, under = levels - 1, levels - 2
 
     def bit_of(level):
         return lax.rem(seq // (1 << level), 2)
 
+    def flipped(level):
+        return (1 << level) - 2 * (1 << level) * bit_of(level)
+
     def sibling(level):
-        return seq + (1 << level) - 2 * (1 << level) * bit_of(level)
+        return seq + flipped(level)
+
+    cousin = seq + flipped(top) + flipped(under)
+    upper = bit_of(top) == 1
+    far = bit_of(under) == 1
+    is_ll = (bit_of(top) == 0) & (bit_of(under) == 0)
+    is_lr = (bit_of(top) == 0) & (bit_of(under) == 1)
+    is_ul = (bit_of(top) == 1) & (bit_of(under) == 0)
+    is_ur = (bit_of(top) == 1) & (bit_of(under) == 1)
 
     barrier = pltpu.get_barrier_semaphore()
     for offset in range(1, feats):
         pl.semaphore_signal(
             barrier, inc=1, device_id=(seq, lax.rem(feat + offset, feats)), device_id_type=MESH
         )
-    for level in range(levels):
-        pl.semaphore_signal(
-            barrier, inc=1, device_id=(sibling(level), feat), device_id_type=MESH
+    for other in [sibling(level) for level in range(levels)] + [cousin]:
+        pl.semaphore_signal(barrier, inc=1, device_id=(other, feat), device_id_type=MESH)
+    rows = rows_ref[...]
+    at["own_rows"][...] = rows.astype(jnp.float32)
+    local = lax.dot_general(
+        rows, rows, (((1,), (1,)), ((), ())), preferred_element_type=jnp.float32
+    )
+    pl.semaphore_wait(barrier, feats + levels)
+
+    def remote(src, dst, sends, recvs, other):
+        return pltpu.make_async_remote_copy(
+            src_ref=src, dst_ref=dst, send_sem=sends, recv_sem=recvs,
+            device_id=(other, feat), device_id_type=MESH,
         )
-    pl.semaphore_wait(barrier, feats - 1 + levels)
 
     def send_sum(slots, phase):
         copies = []
@@ -212,93 +271,254 @@
             total = total + slots[index]
         return total
 
+    def part(bits):
+        size = RANK >> bits
+        first = 0
+        for bit in range(bits):
+            first = first + bit_of(bit) * (RANK >> (bit + 1))
+        return pl.ds(pl.multiple_of(first, size), size) if bits else pl.ds(0, RANK)
+
     def fetch(level):
         for index, hop in enumerate(range(level, -1, -1)):
             source = tree if hop == level else partner
-            bits = hop if hop == level else hop + 1
-            size = RANK >> bits
-            first = 0
-            for bit in range(bits):
-                first = first + bit_of(bit) * (RANK >> (bit + 1))
-            span = pl.ds(pl.multiple_of(first, size), size) if bits else pl.ds(0, RANK)
-            copy = pltpu.make_async_remote_copy(
-                src_ref=source.at[level, span],
-                dst_ref=partner.at[level, span],
-                send_sem=pair_send.at[level, index],
-                recv_sem=pair_recv.at[level, index],
-                device_id=(sibling(hop), feat),
-                device_id_type=MESH,
+            span = part(hop if hop == level else hop + 1)
+            copy = remote(
+                source.at[level, span], partner.at[level, span],
+                pair_send.at[level, index], pair_recv.at[level, index], sibling(hop),
             )
             copy.start()
             copy.wait()
 
-    rows = rows_ref[...]
-    slab_slots[feat] = lax.dot_general(
-        rows, rows, (((1,), (1,)), ((), ())), preferred_element_type=jnp.float32
-    )
-    gram = finish_sum(slab_slots, send_sum(slab_slots, 0))
-    ((mixing, own_gram),) = reduce_grams([gram], work)
-    h, m, l = split_3(mixing)
-    sketch = (
-        jnp.dot(l, rows, preferred_element_type=jnp.float32)
-        + jnp.dot(m, rows, preferred_element_type=jnp.float32)
-        + jnp.dot(h, rows, preferred_element_type=jnp.float32)
-    )
-    tree[0, :, :width] = sketch
-    tree[0, :, width:] = own_gram
-    prefix[...] = sketch
-    prefix_gram = own_gram
-
-    for level in range(levels):
+    parity = bit_of(0)
+    rows_copy = remote(
+        at["own_rows"], at["other_rows"], core_send.at[0], core_recv.at[0], sibling(0)
+    )
+    rows_copy.start()
+    slab_slots, cross_slots, cross_full = at["slab_slots"], at["cross_slots"], at["cross_full"]
+    both, between, diagonal = fold(local)
+    slab_slots[feat, :RANK] = both
+    slab_slots[feat, RANK : 2 * RANK] = between
+    slab_slots[feat, 2 * RANK :] = diagonal
+    slab_copies = send_sum(slab_slots, 0)
+    rows_copy.wait()
+    other_rows = at["other_rows"][...].astype(jnp.bfloat16)
+    half = jnp.where(
+        parity == 0, at["own_rows"][:RANK], at["other_rows"][RANK:]
+    ).astype(jnp.bfloat16)
+    odd_rows = jnp.where(parity == 0, at["other_rows"][...], at["own_rows"][...]).astype(jnp.bfloat16)
+    cross_slots[feat] = lax.dot_general(
+        half, odd_rows, (((1,), (1,)), ((), ())), preferred_element_type=jnp.float32
+    )
+    cross_copies = send_sum(cross_slots, 1)
+    packed = finish_sum(slab_slots, slab_copies)
+    gram = unfold(packed[:RANK], packed[RANK : 2 * RANK], packed[2 * RANK : 2 * RANK + 1])
+
+    share = remote(
+        cross_full.at[parity], cross_full.at[parity], core_send.at[1], core_recv.at[1], sibling(0)
+    )
+
+    def share_cross():
+        cross_full[parity] = finish_sum(cross_slots, cross_copies)
+        share.start()
+
+    ((mixing, own_gram),) = reduce_grams([gram], work, share_cross)
+    mixes = at["mixes"]
+    mixes[parity, :, : 2 * RANK] = mixing
+    mixes[parity, :, 2 * RANK :] = own_gram
+    swap = remote(mixes.at[parity], mixes.at[parity], core_send.at[2], core_recv.at[2], sibling(0))
+    swap.start()
+    prefix[...] = mix_rows(mixing, rows)
+    share.wait()
+    swap.wait()
+    even, odd = mixes[0, :, : 2 * RANK], mixes[1, :, : 2 * RANK]
+    crossed = jnp.concatenate([cross_full[0], cross_full[1]], 0)
+    crossed = mm_t(mm(even, crossed), odd)
+    ((mixing, new_gram),) = reduce_grams(
+        [stack(mixes[0, :, 2 * RANK :], crossed, mixes[1, :, 2 * RANK :])], work
+    )
+    even, odd = mm(mixing[:, :RANK], even), mm(mixing[:, RANK:], odd)
+    block = mix_rows(jnp.where(parity == 0, even, odd), rows) + mix_rows(
+        jnp.where(parity == 0, odd, even), other_rows
+    )
+    tree[1, :, :width] = block
+    tree[1, :, width:] = new_gram
+    prefix[...] = jnp.where(parity == 1, block, prefix[...])
+    prefix_gram[...] = jnp.where(parity == 1, new_gram, own_gram)
+
+    mine = part(under)
+    size = RANK >> under
+    near = [pl.ds(pl.multiple_of(mine.start + piece * (size // 2), size // 2), size // 2) for piece in range(2)]
+
+    def lift(index, source, span, slot, other):
+        return remote(
+            source, lower.at[slot, span], up_send.at[index], up_recv.at[index], other
+        )
+
+    send_right = lift(0, tree.at[under, mine, pl.ds(0, width)], mine, 1, cousin)
+    send_left = [
+        lift(1 + piece, partner.at[under, near[piece], pl.ds(0, width)], near[piece], 0, cousin)
+        for piece in range(2)
+    ]
+    pass_right = lift(3, lower.at[1, mine], mine, 1, sibling(under))
+    pass_left = [
+        lift(4 + piece, lower.at[0, near[piece]], near[piece], 0, sibling(under))
+        for piece in range(2)
+    ]
+
+    for level in range(1, top):
+        last = level == under
+        if last:
+            @pl.when(is_lr)
+            def _():
+                send_right.start()
+
         fetch(level)
-        slots = level_slots[level]
-        with_prefix = level > 0
-        with_tree = level + 1 < levels or level == 0
-        lefts = []
-        if with_tree:
-            lefts.append((tree.at[level, :, :width], tree[level, :, width:]))
-        if with_prefix:
-            lefts.append((prefix, prefix_gram))
+        if last:
+            @pl.when(is_lr)
+            def _():
+                for copy in send_left:
+                    copy.start()
+
+            @pl.when(is_ul)
+            def _():
+                send_right.wait_recv()
+                pass_right.start()
+
+        other = partner[level, :, :width]
+        other_gram = partner[level, :, width:]
+        lefts = [(tree[level, :, :width], tree[level, :, width:]), (prefix[...], prefix_gram[...])]
+        if last:
+            full = bit_of(0)
+            for bit in range(1, level):
+                full = full * bit_of(bit)
+            own = far & (full == 0)
+            lefts = [tuple(jnp.where(own, mine_, tree_) for tree_, mine_ in zip(*lefts))]
+        slots = at["level_slots"] if last else at["twin_slots"].at[level - 1]
         for index, (left, _) in enumerate(lefts):
-            slots[feat, index * RANK : (index + 1) * RANK, :] = mm_t(
-                left[...], partner[level, :, :width]
-            )
+            slots[feat, index * RANK : (index + 1) * RANK, :] = mm_t(left, other)
         crosses = finish_sum(slots, send_sum(slots, 1 + level))
-        other = partner[level, :, width:]
-        stacked = []
-        for index, (_, left_gram) in enumerate(lefts):
-            cross = crosses[index * RANK : (index + 1) * RANK]
-            stacked.append(
-                jnp.concatenate(
+
+        def pass_on():
+            @pl.when(is_ul)
+            def _():
+                send_left[1].wait_recv()
+                pass_left[1].start()
+
+        if last:
+            @pl.when(is_ul)
+            def _():
+                send_left[0].wait_recv()
+                pass_left[0].start()
+
+        results = reduce_grams(
+            [
+                stack(left_gram, crosses[index * RANK : (index + 1) * RANK], other_gram)
+                for index, (_, left_gram) in enumerate(lefts)
+            ],
+            work,
+            pass_on if last else None,
+        )
+        if last:
+            sent, got = at["top_sent"], at["top_got"]
+            sent[:, : 2 * RANK] = results[0][0]
+            sent[:, 2 * RANK :] = results[0][1]
+            above = [
+                remote(sent, got, up_send.at[6], up_recv.at[6], seq + flipped(top) + flipped(under)),
+                remote(sent, got, up_send.at[7], up_recv.at[6], seq + flipped(top)),
+            ]
+
+            @pl.when(is_ll)
+            def _():
+                for copy in above:
+                    copy.start()
+
+            @pl.when(is_ur)
+            def _():
+                pass_right.wait_recv()
+                for copy in pass_left:
+                    copy.wait_recv()
+
+            shares = []
+            for hop in range(under - 1, -1, -1):
+                shares.append(
                     [
-                        jnp.concatenate([left_gram, cross], 1),
-                        jnp.concatenate([cross.T, other], 1),
-                    ],
-                    0,
+                        remote(
+                            lower.at[slot, part(hop + 1)], lower.at[slot, part(hop + 1)],
+                            share_send.at[slot, hop], share_recv.at[slot, hop], sibling(hop),
+                        )
+                        for slot in range(2)
+                    ]
                 )
-            )
-        results = reduce_grams(stacked, work)
-        merged = []
-        for (left, _), (mixing, new_gram) in zip(lefts, results):
-            merged.append(
-                (mm(mixing[:, :RANK], left[...]) + mm(mixing[:, RANK:], partner[level, :, :width]), new_gram)
-            )
+
+            @pl.when(upper)
+            def _():
+                for copy in shares[0]:
+                    copy.start()
+
+        merged = [
+            (mm(mixing[:, :RANK], left) + mm(mixing[:, RANK:], other), new_gram)
+            for (left, _), (mixing, new_gram) in zip(lefts, results)
+        ]
         keep = bit_of(level) == 1
         prefix[...] = jnp.where(keep, merged[-1][0], prefix[...])
-        prefix_gram = jnp.where(keep, merged[-1][1], prefix_gram)
-        if level + 1 < levels:
+        prefix_gram[...] = jnp.where(keep, merged[-1][1], prefix_gram[...])
+        if not last:
             tree[level + 1, :, :width] = merged[0][0]
             tree[level + 1, :, width:] = merged[0][1]
+
+    @pl.when(is_lr)
+    def _():
+        send_right.wait_send()
+        for copy in send_left:
+            copy.wait_send()
+
+    @pl.when(is_ll)
+    def _():
+        for copy in above:
+            copy.wait_send()
+
+    @pl.when(is_ul)
+    def _():
+        pass_right.wait_send()
+        for copy in pass_left:
+            copy.wait_send()
+
+    @pl.when(upper)
+    def _():
+        for index, pair in enumerate(shares):
+            if index:
+                for copy in pair:
+                    copy.start()
+            for copy in pair:
+                copy.wait()
+        slots = at["top_slots"]
+        for slot in range(2):
+            slots[feat, slot * RANK : (slot + 1) * RANK, :] = mm_t(lower[slot], prefix[...])
+        copies = send_sum(slots, 1 + top)
+        above[0].wait_recv()
+        got = at["top_got"]
+        mixed = got[:, : 2 * RANK]
+        crossed = mm(mixed, finish_sum(slots, copies))
+        ((mixing, new_gram),) = reduce_grams(
+            [stack(got[:, 2 * RANK :], crossed, prefix_gram[...])], work
+        )
+        mixed = mm(mixing[:, :RANK], mixed)
+        prefix[...] = (
+            mm(mixed[:, :RANK], lower[0])
+            + mm(mixed[:, RANK:], lower[1])
+            + mm(mixing[:, RANK:], prefix[...])
+        )
+        prefix_gram[...] = new_gram
 
     ridge = ridge_ref[0, 0]
     seen_rows = ((seq + 1) * rows_ref.shape[0]).astype(jnp.float32)
     seen = jnp.full((1, 1), seen_rows * ridge, jnp.float32)
     half_basis = (prefix[...] * lax.rsqrt(seen)).astype(jnp.bfloat16)
-    last_slots[feat] = lax.dot_general(
+    at["last_slots"][feat] = lax.dot_general(
         rows, half_basis, (((1,), (1,)), ((), ())), preferred_element_type=jnp.float32
     )
-    copies = send_sum(last_slots, 1 + levels)
-    shifted = eye() + prefix_gram / seen
+    copies = send_sum(at["last_slots"], 1 + levels)
+    shifted = eye() + prefix_gram[...] / seen
     norm = jnp.sqrt(
         jnp.sum(jnp.sum(shifted * shifted, axis=1, keepdims=True), axis=0, keepdims=True)
     )
@@ -318,7 +538,7 @@
     total_gram = shifted + current * jnp.sqrt(norm)
     total_gram = 0.5 * (total_gram + total_gram.T)
     (inverse,) = factorize([total_gram], work)
-    projection = finish_sum(last_slots, copies)
+    projection = finish_sum(at["last_slots"], copies)
     coefficients = mm(mm_t(projection, inverse), inverse).astype(jnp.bfloat16)
     restored = jnp.dot(coefficients, half_basis, preferred_element_type=jnp.float32)
     out_ref[...] = (
@@ -330,34 +550,48 @@
     tokens, width = activations.shape
     feats = lax.axis_size("feat")
     levels = lax.axis_size("seq").bit_length() - 1
-    wide = (RANK, width)
     f32 = jnp.float32
-    scratch = [
-        pltpu.VMEM((2, RANK, 2 * RANK), f32),
-        pltpu.VMEM((levels, RANK, width + RANK), f32),
-        pltpu.VMEM(wide, f32),
-        pltpu.VMEM((levels, RANK, width + RANK), f32),
-        pltpu.VMEM((feats, tokens, tokens), f32),
-    ]
-    for level in range(levels):
-        count = 2 if 0 < level < levels - 1 else 1
-        scratch.append(pltpu.VMEM((feats, count * RANK, RANK), f32))
-    scratch.append(pltpu.VMEM((feats, tokens, RANK), f32))
-    scratch += [
-        pltpu.SemaphoreType.DMA((levels + 2, feats)),
-        pltpu.SemaphoreType.DMA((levels + 2, feats)),
-        pltpu.SemaphoreType.DMA((levels, levels)),
-        pltpu.SemaphoreType.DMA((levels, levels)),
-    ]
+    dma = pltpu.SemaphoreType.DMA
+    scratch = dict(
+        work=pltpu.VMEM((2, RANK, 2 * RANK), f32),
+        tree=pltpu.VMEM((levels - 1, RANK, width + RANK), f32),
+        partner=pltpu.VMEM((levels - 1, RANK, width + RANK), f32),
+        prefix=pltpu.VMEM((RANK, width), f32),
+        prefix_gram=pltpu.VMEM((RANK, RANK), f32),
+        lower=pltpu.VMEM((2, RANK, width), f32),
+        own_rows=pltpu.VMEM((tokens, width), f32),
+        other_rows=pltpu.VMEM((tokens, width), f32),
+        slab_slots=pltpu.VMEM((feats, 2 * RANK + 8, RANK), f32),
+        cross_slots=pltpu.VMEM((feats, RANK, 2 * RANK), f32),
+        cross_full=pltpu.VMEM((2, RANK, 2 * RANK), f32),
+        mixes=pltpu.VMEM((2, RANK, 3 * RANK), f32),
+        level_slots=pltpu.VMEM((feats, RANK, RANK), f32),
+        top_sent=pltpu.VMEM((RANK, 3 * RANK), f32),
+        top_got=pltpu.VMEM((RANK, 3 * RANK), f32),
+        top_slots=pltpu.VMEM((feats, 2 * RANK, RANK), f32),
+        last_slots=pltpu.VMEM((feats, tokens, RANK), f32),
+        send_sem=dma((levels + 2, feats)),
+        recv_sem=dma((levels + 2, feats)),
+        pair_send=dma((levels, levels)),
+        pair_recv=dma((levels, levels)),
+        core_send=dma((3,)),
+        core_recv=dma((3,)),
+        up_send=dma((8,)),
+        up_recv=dma((8,)),
+        share_send=dma((2, levels)),
+        share_recv=dma((2, levels)),
+    )
+    if levels > 3:
+        scratch["twin_slots"] = pltpu.VMEM((levels - 3, feats, 2 * RANK, RANK), f32)
     return pl.pallas_call(
-        functools.partial(kernel, levels, feats),
+        functools.partial(kernel, levels, feats, tuple(scratch)),
         out_shape=jax.ShapeDtypeStruct(activations.shape, activations.dtype),
         in_specs=[
             pl.BlockSpec(memory_space=pltpu.SMEM),
             pl.BlockSpec(memory_space=pltpu.VMEM),
         ],
         out_specs=pl.BlockSpec(memory_space=pltpu.VMEM),
-        scratch_shapes=scratch,
+        scratch_shapes=list(scratch.values()),
         compiler_params=pltpu.CompilerParams(
             collective_id=0, has_side_effects=True, vmem_limit_bytes=60 * 1024 * 1024
         ),

time: 140 us -> 111 us (0.79)
  the two profiles are of different devices: /device:TPU:0 before, /device:TPU:24 now
where the time goes in v2:
time: 111 us
  Pallas kernels  108 us (97%)
  local copies, waits for them, and re-layouts  2.06 us (2%)
    pallas_call x1, Pallas kernels, on_device(): pl.pallas_call(functools.partial(kernel, levels, feats, tuple(scratch)),...  108 us

profile of v2, /device:TPU:24, one launch (start us, length us, event | category | flops | bytes accessed | tf_op | source)
XLA Modules:
  0.0 110.7 jit_solution(11974190307307726005)
XLA Ops:
  0.7 107.9 %shard_map.28 = bf16[256,1536]{1,0:T(8,128)(2,1)} custom-call(f32[1,1]{1,0:T(1,128)} %bitcast.1.ridge_ref, bf16[256,1536]{1,0:T(8,128)(2,1)} %rows_ref.1), custom_call_target="tpu_custom_call" | custom-call | tf_op jit(solution)/shard_map/pallas_call | solution.py:586
  108.6 2.1 %copy.5 = bf16[256,1536]{1,0:T(8,128)(2,1)} copy(bf16[256,1536]{1,0:T(8,128)(2,1)} %shard_map.28) | data formatting | bytes 1572864

commit v3 on v2

--- a/solution.py
+++ b/solution.py
@@ -23,6 +23,23 @@
     return lax.dot_general(
         a, b, (((1,), (1,)), ((), ())), precision=HIGHEST, preferred_element_type=jnp.float32
     )
+
+
+def mm_square(a, b):
+    a_high, a_middle, a_low = split_3(a)
+    b_high, b_middle, b_low = split_3(b)
+    pair = jnp.concatenate([b_high, b_middle], 1)
+    both = jnp.dot(
+        jnp.concatenate([a_high, a_middle], 1),
+        jnp.concatenate([pair, pair], 0),
+        preferred_element_type=jnp.float32,
+    )
+    rest = jnp.dot(
+        jnp.concatenate([a_high, a_low], 1),
+        jnp.concatenate([b_low, b_high], 0),
+        preferred_element_type=jnp.float32,
+    )
+    return both[:, :RANK] + (both[:, RANK:] + rest)
 
 
 def split_3(x):
@@ -129,7 +146,7 @@
                 a, b, c = split_3(whole)
                 h, m, l = (jnp.where(wide >= first + BLOCK, part.astype(jnp.float32), 0.0) for part in (a, b, c))
                 lhs = jnp.concatenate([h, h, m, m, h, l, jnp.zeros((2 * BLOCK, RANK), jnp.float32)], axis=0)
-                lhs = lhs.T.astype(jnp.bfloat16)
+                lhs = lhs.astype(jnp.bfloat16).T
                 rhs = jnp.concatenate([a, b, a, b, c, a, jnp.zeros((2 * BLOCK, RANK), jnp.bfloat16)], axis=0)
                 update = jnp.dot(lhs, rhs, preferred_element_type=jnp.float32)
                 old = work[k, :, :RANK]
@@ -173,6 +190,32 @@
     )
 
 
+def split_2(x):
+    high = x.astype(jnp.bfloat16)
+    return high, (x - high.astype(jnp.float32)).astype(jnp.bfloat16)
+
+
+def blend(mixing, block):
+    a, b = split_2(mixing)
+    c, d = split_2(block)
+    return (
+        jnp.dot(b, c, preferred_element_type=jnp.float32)
+        + jnp.dot(a, d, preferred_element_type=jnp.float32)
+        + jnp.dot(a, c, preferred_element_type=jnp.float32)
+    )
+
+
+def overlap(first, second):
+    a, b = split_2(first)
+    c, d = split_2(second)
+    dims = (((1,), (1,)), ((), ()))
+    return (
+        lax.dot_general(b, c, dims, preferred_element_type=jnp.float32)
+        + lax.dot_general(a, d, dims, preferred_element_type=jnp.float32)
+        + lax.dot_general(a, c, dims, preferred_element_type=jnp.float32)
+    )
+
+
 def stack(first, cross, last):
     return jnp.concatenate(
         [jnp.concatenate([first, cross], 1), jnp.concatenate([cross.T, last], 1)], 0
@@ -294,6 +337,30 @@
         at["own_rows"], at["other_rows"], core_send.at[0], core_recv.at[0], sibling(0)
     )
     rows_copy.start()
+    far_rows = at["far_rows"]
+    pieces = far_rows.shape[1] // at["far_send"].shape[1]
+    far_copies, far_shares = [], []
+    for piece in range(at["far_send"].shape[1]):
+        span = pl.ds(piece * pieces, pieces)
+        far_copies.append(
+            remote(
+                at["own_rows"].at[span], far_rows.at[parity, span],
+                at["far_send"].at[0, piece], at["far_recv"].at[0, piece], sibling(1),
+            )
+        )
+        far_shares.append(
+            remote(
+                far_rows.at[parity, span], far_rows.at[parity, span],
+                at["far_send"].at[1, piece], at["far_recv"].at[1, piece], sibling(0),
+            )
+        )
+    for copy in far_copies:
+        copy.start()
+
+    def share_far(piece):
+        far_copies[piece].wait()
+        far_shares[piece].start()
+
     slab_slots, cross_slots, cross_full = at["slab_slots"], at["cross_slots"], at["cross_full"]
     both, between, diagonal = fold(local)
     slab_slots[feat, :RANK] = both
@@ -327,6 +394,7 @@
     mixes[parity, :, 2 * RANK :] = own_gram
     swap = remote(mixes.at[parity], mixes.at[parity], core_send.at[2], core_recv.at[2], sibling(0))
     swap.start()
+    share_far(0)
     prefix[...] = mix_rows(mixing, rows)
     share.wait()
     swap.wait()
@@ -334,9 +402,24 @@
     crossed = jnp.concatenate([cross_full[0], cross_full[1]], 0)
     crossed = mm_t(mm(even, crossed), odd)
     ((mixing, new_gram),) = reduce_grams(
-        [stack(mixes[0, :, 2 * RANK :], crossed, mixes[1, :, 2 * RANK :])], work
+        [stack(mixes[0, :, 2 * RANK :], crossed, mixes[1, :, 2 * RANK :])],
+        work,
+        functools.partial(share_far, 1),
     )
     even, odd = mm(mixing[:, :RANK], even), mm(mixing[:, RANK:], odd)
+    turns, far_turns = at["turns"], at["far_turns"]
+    turns[:, : 2 * RANK] = even
+    turns[:, 2 * RANK : 4 * RANK] = odd
+    turns[:, 4 * RANK :] = new_gram
+    turn_copies = [
+        remote(
+            source.at[part(1)], far_turns.at[part(1)], core_send.at[3 + hop], core_recv.at[3 + hop], sibling(hop)
+        )
+        for hop, source in ((1, turns), (0, far_turns))
+    ]
+    turn_copies[0].start()
+    for piece in range(2, len(far_copies)):
+        share_far(piece)
     block = mix_rows(jnp.where(parity == 0, even, odd), rows) + mix_rows(
         jnp.where(parity == 0, odd, even), other_rows
     )
@@ -347,129 +430,155 @@
 
     mine = part(under)
     size = RANK >> under
-    near = [pl.ds(pl.multiple_of(mine.start + piece * (size // 2), size // 2), size // 2) for piece in range(2)]
+    count = min(4, size // 8)
+    size = size // count
+    near = [pl.ds(pl.multiple_of(mine.start + piece * size, size), size) for piece in range(count)]
 
     def lift(index, source, span, slot, other):
         return remote(
             source, lower.at[slot, span], up_send.at[index], up_recv.at[index], other
         )
 
-    send_right = lift(0, tree.at[under, mine, pl.ds(0, width)], mine, 1, cousin)
+    send_right = [
+        lift(piece, tree.at[under, near[piece], pl.ds(0, width)], near[piece], 1, cousin)
+        for piece in range(count)
+    ]
     send_left = [
-        lift(1 + piece, partner.at[under, near[piece], pl.ds(0, width)], near[piece], 0, cousin)
-        for piece in range(2)
+        lift(4 + piece, partner.at[under, near[piece], pl.ds(0, width)], near[piece], 0, cousin)
+        for piece in range(count)
     ]
-    pass_right = lift(3, lower.at[1, mine], mine, 1, sibling(under))
+    pass_right = [
+        lift(8 + piece, lower.at[1, near[piece]], near[piece], 1, sibling(under))
+        for piece in range(count)
+    ]
     pass_left = [
-        lift(4 + piece, lower.at[0, near[piece]], near[piece], 0, sibling(under))
-        for piece in range(2)
+        lift(12 + piece, lower.at[0, near[piece]], near[piece], 0, sibling(under))
+        for piece in range(count)
     ]
-
-    for level in range(1, top):
-        last = level == under
-        if last:
-            @pl.when(is_lr)
-            def _():
-                send_right.start()
-
-        fetch(level)
-        if last:
-            @pl.when(is_lr)
-            def _():
-                for copy in send_left:
-                    copy.start()
-
-            @pl.when(is_ul)
-            def _():
-                send_right.wait_recv()
-                pass_right.start()
-
+    sent, got = at["top_sent"], at["top_got"]
+    above = [
+        remote(sent.at[mine], got.at[mine], up_send.at[16 + index], up_recv.at[16], other)
+        for index, other in enumerate((cousin, sibling(top)))
+    ]
+    shares = [
+        [
+            remote(
+                ref.at[part(hop + 1)], ref.at[part(hop + 1)],
+                share_send.at[slot, hop], share_recv.at[slot, hop], sibling(hop),
+            )
+            for slot, ref in enumerate((lower.at[0], lower.at[1], got))
+        ]
+        for hop in range(under - 1, -1, -1)
+    ]
+
+    def receive(level):
+        if level > 1:
+            fetch(level)
+            return
+        turn_copies[0].wait()
+        turn_copies[1].start()
+        for copy in far_shares:
+            copy.wait()
+        turn_copies[1].wait()
+        partner[1, :, :width] = mix_rows(
+            far_turns[:, : 2 * RANK], far_rows[0].astype(jnp.bfloat16)
+        ) + mix_rows(far_turns[:, 2 * RANK : 4 * RANK], far_rows[1].astype(jnp.bfloat16))
+        partner[1, :, width:] = far_turns[:, 4 * RANK :]
+
+    for level in range(1, under):
+        receive(level)
         other = partner[level, :, :width]
         other_gram = partner[level, :, width:]
         lefts = [(tree[level, :, :width], tree[level, :, width:]), (prefix[...], prefix_gram[...])]
-        if last:
-            full = bit_of(0)
-            for bit in range(1, level):
-                full = full * bit_of(bit)
-            own = far & (full == 0)
-            lefts = [tuple(jnp.where(own, mine_, tree_) for tree_, mine_ in zip(*lefts))]
-        slots = at["level_slots"] if last else at["twin_slots"].at[level - 1]
+        slots = at["twin_slots"].at[level - 1]
         for index, (left, _) in enumerate(lefts):
-            slots[feat, index * RANK : (index + 1) * RANK, :] = mm_t(left, other)
+            slots[feat, index * RANK : (index + 1) * RANK, :] = overlap(left, other)
         crosses = finish_sum(slots, send_sum(slots, 1 + level))
-
-        def pass_on():
-            @pl.when(is_ul)
-            def _():
-                send_left[1].wait_recv()
-                pass_left[1].start()
-
-        if last:
-            @pl.when(is_ul)
-            def _():
-                send_left[0].wait_recv()
-                pass_left[0].start()
-
         results = reduce_grams(
             [
                 stack(left_gram, crosses[index * RANK : (index + 1) * RANK], other_gram)
                 for index, (_, left_gram) in enumerate(lefts)
             ],
             work,
-            pass_on if last else None,
-        )
-        if last:
-            sent, got = at["top_sent"], at["top_got"]
-            sent[:, : 2 * RANK] = results[0][0]
-            sent[:, 2 * RANK :] = results[0][1]
-            above = [
-                remote(sent, got, up_send.at[6], up_recv.at[6], seq + flipped(top) + flipped(under)),
-                remote(sent, got, up_send.at[7], up_recv.at[6], seq + flipped(top)),
-            ]
-
-            @pl.when(is_ll)
-            def _():
-                for copy in above:
-                    copy.start()
-
-            @pl.when(is_ur)
-            def _():
-                pass_right.wait_recv()
-                for copy in pass_left:
-                    copy.wait_recv()
-
-            shares = []
-            for hop in range(under - 1, -1, -1):
-                shares.append(
-                    [
-                        remote(
-                            lower.at[slot, part(hop + 1)], lower.at[slot, part(hop + 1)],
-                            share_send.at[slot, hop], share_recv.at[slot, hop], sibling(hop),
-                        )
-                        for slot in range(2)
-                    ]
-                )
-
-            @pl.when(upper)
-            def _():
-                for copy in shares[0]:
-                    copy.start()
-
+        )
         merged = [
-            (mm(mixing[:, :RANK], left) + mm(mixing[:, RANK:], other), new_gram)
+            (blend(mixing, jnp.concatenate([left, other], 0)), new_gram)
             for (left, _), (mixing, new_gram) in zip(lefts, results)
         ]
         keep = bit_of(level) == 1
-        prefix[...] = jnp.where(keep, merged[-1][0], prefix[...])
-        prefix_gram[...] = jnp.where(keep, merged[-1][1], prefix_gram[...])
-        if not last:
-            tree[level + 1, :, :width] = merged[0][0]
-            tree[level + 1, :, width:] = merged[0][1]
+        prefix[...] = jnp.where(keep, merged[1][0], prefix[...])
+        prefix_gram[...] = jnp.where(keep, merged[1][1], prefix_gram[...])
+        tree[level + 1, :, :width] = merged[0][0]
+        tree[level + 1, :, width:] = merged[0][1]
 
     @pl.when(is_lr)
     def _():
-        send_right.wait_send()
+        for copy in send_right:
+            copy.start()
+
+    receive(under)
+
+    @pl.when(is_lr)
+    def _():
         for copy in send_left:
+            copy.start()
+
+    @pl.when(is_ul)
+    def _():
+        for copy, later in zip(send_right, pass_right):
+            copy.wait_recv()
+            later.start()
+        shares[0][1].start()
+        for copy, later in zip(send_left, pass_left):
+            copy.wait_recv()
+            later.start()
+        shares[0][0].start()
+
+    @pl.when(jnp.logical_not(is_ul))
+    def _():
+        other = partner[under, :, :width]
+        full = bit_of(0)
+        for bit in range(1, under):
+            full = full * bit_of(bit)
+        own = far & (full == 0)
+        left = jnp.where(own, prefix[...], tree[under, :, :width])
+        left_gram = jnp.where(own, prefix_gram[...], tree[under, :, width:])
+        slots = at["level_slots"]
+        slots[feat] = overlap(left, other)
+        crossed = finish_sum(slots, send_sum(slots, top))
+
+        def share_right():
+            @pl.when(is_ur)
+            def _():
+                for copy in pass_right:
+                    copy.wait_recv()
+                shares[0][1].start()
+
+        ((mixing, new_gram),) = reduce_grams(
+            [stack(left_gram, crossed, partner[under, :, width:])], work, share_right
+        )
+        sent[:, : 2 * RANK] = mixing
+        sent[:, 2 * RANK :] = new_gram
+
+        @pl.when(is_ll)
+        def _():
+            for copy in above:
+                copy.start()
+
+        @pl.when(is_ur)
+        def _():
+            for copy in pass_left:
+                copy.wait_recv()
+            shares[0][0].start()
+
+        @pl.when(far)
+        def _():
+            prefix[...] = blend(mixing, jnp.concatenate([left, other], 0))
+            prefix_gram[...] = new_gram
+
+    @pl.when(is_lr)
+    def _():
+        for copy in send_right + send_left:
             copy.wait_send()
 
     @pl.when(is_ll)
@@ -479,34 +588,37 @@
 
     @pl.when(is_ul)
     def _():
-        pass_right.wait_send()
-        for copy in pass_left:
+        for copy in pass_right + pass_left:
             copy.wait_send()
 
     @pl.when(upper)
     def _():
-        for index, pair in enumerate(shares):
-            if index:
-                for copy in pair:
-                    copy.start()
-            for copy in pair:
-                copy.wait()
         slots = at["top_slots"]
-        for slot in range(2):
-            slots[feat, slot * RANK : (slot + 1) * RANK, :] = mm_t(lower[slot], prefix[...])
-        copies = send_sum(slots, 1 + top)
+        copies = [None, None]
+        for slot in (1, 0):
+            for index, group in enumerate(shares):
+                if index:
+                    group[slot].start()
+                group[slot].wait()
+            slots[slot, feat] = overlap(lower[slot], prefix[...])
+            copies[slot] = send_sum(slots.at[slot], 1 + top + 2 * slot)
         above[0].wait_recv()
-        got = at["top_got"]
+        for index, group in enumerate(shares):
+            group[2].start()
+            if index == 0:
+                crossed = jnp.concatenate(
+                    [finish_sum(slots.at[slot], copies[slot]) for slot in range(2)], 0
+                )
+            group[2].wait()
         mixed = got[:, : 2 * RANK]
-        crossed = mm(mixed, finish_sum(slots, copies))
+        crossed = mm(mixed, crossed)
         ((mixing, new_gram),) = reduce_grams(
             [stack(got[:, 2 * RANK :], crossed, prefix_gram[...])], work
         )
         mixed = mm(mixing[:, :RANK], mixed)
-        prefix[...] = (
-            mm(mixed[:, :RANK], lower[0])
-            + mm(mixed[:, RANK:], lower[1])
-            + mm(mixing[:, RANK:], prefix[...])
+        prefix[...] = blend(
+            jnp.concatenate([mixed, mixing[:, RANK:]], 1),
+            jnp.concatenate([lower[0], lower[1], prefix[...]], 0),
         )
         prefix_gram[...] = new_gram
 
@@ -528,9 +640,9 @@
 
     def root_step(index, carry):
         current, other = work[0, :, :RANK], work[0, :, RANK:]
-        middle = 1.5 * eye() - 0.5 * mm(other, current)
-        work[0, :, :RANK] = mm(current, middle)
-        work[0, :, RANK:] = mm(middle, other)
+        middle = 1.5 * eye() - 0.5 * mm_square(other, current)
+        work[0, :, :RANK] = mm_square(current, middle)
+        work[0, :, RANK:] = mm_square(middle, other)
         return carry
 
     lax.fori_loop(0, ROOT_STEPS, root_step, 0)
@@ -562,24 +674,29 @@
         own_rows=pltpu.VMEM((tokens, width), f32),
         other_rows=pltpu.VMEM((tokens, width), f32),
         slab_slots=pltpu.VMEM((feats, 2 * RANK + 8, RANK), f32),
+        far_rows=pltpu.VMEM((2, tokens, width), f32),
+        turns=pltpu.VMEM((RANK, 5 * RANK), f32),
+        far_turns=pltpu.VMEM((RANK, 5 * RANK), f32),
         cross_slots=pltpu.VMEM((feats, RANK, 2 * RANK), f32),
         cross_full=pltpu.VMEM((2, RANK, 2 * RANK), f32),
         mixes=pltpu.VMEM((2, RANK, 3 * RANK), f32),
         level_slots=pltpu.VMEM((feats, RANK, RANK), f32),
         top_sent=pltpu.VMEM((RANK, 3 * RANK), f32),
         top_got=pltpu.VMEM((RANK, 3 * RANK), f32),
-        top_slots=pltpu.VMEM((feats, 2 * RANK, RANK), f32),
+        top_slots=pltpu.VMEM((2, feats, RANK, RANK), f32),
         last_slots=pltpu.VMEM((feats, tokens, RANK), f32),
-        send_sem=dma((levels + 2, feats)),
-        recv_sem=dma((levels + 2, feats)),
+        send_sem=dma((levels + 3, feats)),
+        recv_sem=dma((levels + 3, feats)),
         pair_send=dma((levels, levels)),
         pair_recv=dma((levels, levels)),
-        core_send=dma((3,)),
-        core_recv=dma((3,)),
-        up_send=dma((8,)),
-        up_recv=dma((8,)),
-        share_send=dma((2, levels)),
-        share_recv=dma((2, levels)),
+        far_send=dma((2, 4)),
+        far_recv=dma((2, 4)),
+        core_send=dma((5,)),
+        core_recv=dma((5,)),
+        up_send=dma((18,)),
+        up_recv=dma((18,)),
+        share_send=dma((3, levels)),
+        share_recv=dma((3, levels)),
     )
     if levels > 3:
         scratch["twin_slots"] = pltpu.VMEM((levels - 3, feats, 2 * RANK, RANK), f32)

time: 111 us -> 98.6 us (0.89)
  Pallas kernels: 108 us -> 95.3 us
    pallas_call x1, Pallas kernels: 108 us -> 95.3 us  [on_device(): pl.pallas_call(functools.partial(kernel, levels, feats, tuple(scratch)),...]
where the time goes in v3:
time: 98.6 us; the launch traced here: 98 us
  Pallas kernels  95.3 us (97%)
  local copies, waits for them, and re-layouts  2.06 us (2%)
    pallas_call x1, Pallas kernels, on_device(): pl.pallas_call(functools.partial(kernel, levels, feats, tuple(scratch)),...  95.3 us
    unnamed x1, local copies, waits for them, and re-layouts  2.06 us

profile of v3, /device:TPU:24, one launch (start us, length us, event | category | flops | bytes accessed | tf_op | source)
XLA Modules:
  0.0 98.0 jit_solution(9288154996375423195)
XLA Ops:
  0.7 95.3 %shard_map.28 = bf16[256,1536]{1,0:T(8,128)(2,1)} custom-call(f32[1,1]{1,0:T(1,128)} %bitcast.1.ridge_ref, bf16[256,1536]{1,0:T(8,128)(2,1)} %rows_ref.1), custom_call_target="tpu_custom_call" | custom-call | tf_op jit(solution)/shard_map/pallas_call | solution.py:703
  95.9 2.1 %copy.5 = bf16[256,1536]{1,0:T(8,128)(2,1)} copy(bf16[256,1536]{1,0:T(8,128)(2,1)} %shard_map.28) | data formatting | bytes 1572864

commit v4 on v3

--- a/solution.py
+++ b/solution.py
@@ -260,6 +260,15 @@
     def flipped(level):
         return (1 << level) - 2 * (1 << level) * bit_of(level)
 
+    def mirror(offset):
+        if feats & (feats - 1):
+            return lax.rem(feat + offset, feats)
+        other = feat
+        for bit in range(feats.bit_length() - 1):
+            if offset >> bit & 1:
+                other = other + (1 << bit) - 2 * (1 << bit) * lax.rem(feat // (1 << bit), 2)
+        return other
+
     def sibling(level):
         return seq + flipped(level)
 
@@ -293,13 +302,13 @@
 
     def send_sum(slots, phase):
         copies = []
-        for offset in range(1, feats):
+        for offset in range(feats - 1, 0, -1):
             copy = pltpu.make_async_remote_copy(
                 src_ref=slots.at[feat],
                 dst_ref=slots.at[feat],
                 send_sem=send_sem.at[phase, offset],
                 recv_sem=recv_sem.at[phase, offset],
-                device_id=(seq, lax.rem(feat + offset, feats)),
+                device_id=(seq, mirror(offset)),
                 device_id_type=MESH,
             )
             copy.start()

time: 98.6 us -> 98.7 us (level)
  no operation moved by 1% of the time
where the time goes in v4:
time: 98.7 us; the launch traced here: 97.9 us
  Pallas kernels  95.2 us (96%)
  local copies, waits for them, and re-layouts  2.06 us (2%)
    pallas_call x1, Pallas kernels, on_device(): pl.pallas_call(functools.partial(kernel, levels, feats, tuple(scratch)),...  95.2 us
    unnamed x1, local copies, waits for them, and re-layouts  2.06 us

profile of v4, /device:TPU:24, one launch (start us, length us, event | category | flops | bytes accessed | tf_op | source)
XLA Modules:
  0.0 97.9 jit_solution(16011145097237972487)
XLA Ops:
  0.7 95.2 %shard_map.28 = bf16[256,1536]{1,0:T(8,128)(2,1)} custom-call(f32[1,1]{1,0:T(1,128)} %bitcast.1.ridge_ref, bf16[256,1536]{1,0:T(8,128)(2,1)} %rows_ref.1), custom_call_target="tpu_custom_call" | custom-call | tf_op jit(solution)/shard_map/pallas_call | solution.py:712
  95.9 2.1 %copy.5 = bf16[256,1536]{1,0:T(8,128)(2,1)} copy(bf16[256,1536]{1,0:T(8,128)(2,1)} %shard_map.28) | data formatting | bytes 1572864
